TPU v7x, 32 devices: a whole 2x2x4 slice. The times are simulated.
32 devices in a mesh: panel: 8 (over z, core), rhs: 4 (over y, x).
Axes of the slice: x: 2, y: 2, z: 4, core: 2. Of those that a mesh axis runs over, the one named last changes fastest.
Arguments:
- pivot_rhs: float32 [2, 2048, 512], P(None, 'panel', 'rhs'), may hold values from -6 to 6
- update_rhs: float32 [4096, 512], P('panel', 'rhs'), may hold values from -6 to 6
- parent_rhs: float32 [4096, 512], P('panel', 'rhs'), may hold values from -6 to 6
- lower_pivot: bfloat16 [2, 2048, 2048], P(None, 'panel', 'rhs'), may hold values from -1 to 1.4, as said below
- lower_update: bfloat16 [4096, 2048], P('panel', 'rhs'), may hold values from -0.125 to 0.125
- parent_lower: bfloat16 [4096, 4096], P('panel', 'rhs'), may hold values from -1 to 1.4, as said below
- parent_upper: bfloat16 [4096, 4096], P('panel', 'rhs'), may hold values from -1 to 1.4, as said below
- upper_pivot: bfloat16 [2, 2048, 2048], P(None, 'panel', 'rhs'), may hold values from -1 to 1.4, as said below
- upper_update: bfloat16 [2, 2048, 2048], P(None, 'panel', 'rhs'), may hold values from -0.125 to 0.125
- maps: int32 [4096], replicated, may hold values from 0 to 4095, as said below
Outputs:
- parent_solution: float32 [4096, 512], P('panel', 'rhs')
- child_solution: float32 [2, 2048, 512], P(None, 'panel', 'rhs')
Inputs may be any that keep to these rules, and one draw needn't show every extreme that they name: `maps`: for each child k, entry k * 2048 + i is 2 * i + b with b equal to 0 or 1; both values of b occur for each child in every draw. `lower_pivot`: each block is lower triangular, diagonal 0.6 to 1.4. `upper_pivot`: each block is upper triangular, diagonal 0.6 to 1.4. `parent_lower`: lower triangular, diagonal 0.6 to 1.4. `parent_upper`: upper triangular, diagonal 0.6 to 1.4.
All inputs are finite; a program needn't handle non-finite values.
Results may differ from a plain program's by a relative error of at most 0.0054.
Values may be sent and summed in bfloat16 or wider, within the bound.
A program may use at most 64 MiB of HBM per device.

v0:
```python
import jax
import jax.numpy as jnp
from jax import lax
from jax.sharding import PartitionSpec as P

F = 4096
FU = 2048


def product(left, right):
    return jnp.dot(left, right, preferred_element_type=jnp.float32)


def paired(left, right):
    return jnp.einsum("kqw,kwr->kqr", left, right, preferred_element_type=jnp.float32)


def through(factor, vector):
    return product(lax.all_gather(factor, "rhs", axis=1, tiled=True), vector)


def shards(
    pivot_rhs,
    update_rhs,
    parent_rhs,
    lower_pivot,
    lower_update,
    parent_lower,
    parent_upper,
    upper_pivot,
    upper_update,
    maps,
):
    panel_index = lax.axis_index("panel")
    row_count = update_rhs.shape[0]
    rhs_width = update_rhs.shape[1]
    pivot_local = pivot_rhs.shape[1]
    first_row = panel_index * row_count
    child_index = first_row // FU
    pivot_all = lax.all_gather(pivot_rhs.astype(jnp.bfloat16), "panel", axis=1, tiled=True)
    own_rhs = lax.dynamic_index_in_dim(pivot_all, child_index, 0, keepdims=False)
    lower_flat = lower_pivot.reshape(2 * pivot_local, lower_pivot.shape[2])
    pieces = (
        lax.all_gather(lower_flat, "rhs", axis=1, tiled=True),
        lax.all_gather(lower_update, "rhs", axis=1, tiled=True),
    )
    width = pieces[0].shape[1]
    blocks = pieces[0].reshape(2, pivot_local, width)
    pivot_mid = paired(blocks, pivot_all)
    update_sum = product(pieces[1], own_rhs)
    update_half = (update_rhs + update_sum).astype(jnp.bfloat16)
    pivot_half = pivot_mid.astype(jnp.bfloat16)
    my_targets = lax.dynamic_slice_in_dim(maps, first_row, row_count, 0)
    select = (lax.broadcasted_iota(jnp.int32, (F, row_count), 0) == my_targets[None, :]).astype(
        jnp.bfloat16
    )
    spread = (
        product(select, update_half)
        .astype(jnp.bfloat16)
        .reshape(F // row_count, row_count, rhs_width)
    )
    received = lax.all_to_all(spread, "panel", split_axis=0, concat_axis=0, tiled=True)
    parent_sum = parent_rhs + jnp.sum(received.astype(jnp.float32), axis=0)
    parent_all = lax.all_gather(parent_sum.astype(jnp.bfloat16), "panel", axis=0, tiled=True)
    parent_mid = through(parent_lower, parent_all)
    middle_all = lax.all_gather(parent_mid.astype(jnp.bfloat16), "panel", axis=0, tiled=True)
    parent_solution = through(parent_upper, middle_all)
    solution_half = parent_solution.astype(jnp.bfloat16)
    pivot_known, solution_all = (
        lax.all_gather(pivot_half, "panel", axis=1, tiled=True),
        lax.all_gather(solution_half, "panel", axis=0, tiled=True),
    )
    remote_rows = jnp.take(solution_all, maps, axis=0).reshape(2, FU, rhs_width)
    pieces = (
        lax.all_gather(upper_pivot, "rhs", axis=2, tiled=True),
        lax.all_gather(upper_update, "rhs", axis=2, tiled=True),
    )
    child_solution = paired(pieces[0], pivot_known) + paired(pieces[1], remote_rows)
    return (parent_solution, child_solution)


def solution(mesh):
    placed = (
        P(None, "panel", "rhs"),
        P("panel", "rhs"),
        P("panel", "rhs"),
        P(None, "panel", "rhs"),
        P("panel", "rhs"),
        P("panel", "rhs"),
        P("panel", "rhs"),
        P(None, "panel", "rhs"),
        P(None, "panel", "rhs"),
        P(),
    )
    return jax.shard_map(
        shards,
        mesh=mesh,
        in_specs=placed,
        out_specs=(P("panel", "rhs"), P(None, "panel", "rhs")),
        check_vma=False,
    )
```

profile of v0, /device:TPU:24, one launch (start us, length us, event | category | flops | bytes accessed | tf_op | source)
XLA Modules:
  0.0 395.7 jit_solution(6019576751417503192)
XLA Ops:
  7.2 0.0 all-gather.12.cloned.1.call-start
  7.2 1.7 convert_element_type.28
  8.9 0.0 all-gather.12.cloned.1.call-update
  8.9 0.0 all-gather.14.cloned.1.call-start
  9.0 0.7 all-gather.14.cloned.1.call-update
  9.7 0.0 all-gather.18.cloned.1.call-start
  9.7 0.7 all-gather.18.cloned.1.call-update
  10.4 0.0 all-gather.16.cloned.1.call-start
  10.5 0.1 dynamic_slice.7
  10.6 21.6 %all-gather.12.cloned.1.call-done = bf16[2,2048,128]{2,1,0:T(8,128)(2,1)} async-done(((bf16[2,256,128]{2,1,0:T(8,128)(2,1)}), bf16[2,2048,128]{2,1,0:T(8,128)(2,1)}) %all-gather.12.cloned.1.call-update) | async-done | bytes 1048592 | tf_op jit(solution)/shard_map/all_gather | solution.py:40
  32.2 37.7 %all-gather.14.cloned.1.call-done = bf16[512,2048]{1,0:T(8,128)(2,1)} async-done(((bf16[512,512]{1,0:T(8,128)(2,1)}), bf16[512,2048]{1,0:T(8,128)(2,1)}) %all-gather.14.cloned.1.call-update) | async-done | bytes 2097168 | tf_op jit(solution)/shard_map/all_gather | solution.py:45
  69.9 3.7 fusion.1
  73.7 29.1 %all_to_all.5 = bf16[8,512,128]{2,1,0:T(8,128)(2,1)S(1)} all-to-all(bf16[8,512,128]{2,1,0:T(8,128)(2,1)S(1)} %bitcast.34), channel_id=1, replica_groups=mesh['panel'=8,'rhs'=4] {'panel'}, dimensions={0} | all-to-all | bytes 2097152 | tf_op jit(solution)/shard_map/all_to_all | solution.py:62
  102.7 0.1 convert_reduce_fusion
  102.9 0.7 add_convert_fusion
  103.6 0.0 all-gather.16.cloned.1.call-update
  103.6 0.0 all-gather.24.cloned.1.call-start
  103.7 0.5 all-gather.24.cloned.1.call-update
  104.2 0.0 all-gather.22.cloned.1.call-start
  104.2 0.5 all-gather.22.cloned.1.call-update
  104.8 0.0 all-gather.20.cloned.1.call-start
  104.8 19.6 %all-gather.18.cloned.1.call-done = bf16[512,4096]{1,0:T(8,128)(2,1)} async-done(((bf16[512,1024]{1,0:T(8,128)(2,1)}), bf16[512,4096]{1,0:T(8,128)(2,1)}) %all-gather.18.cloned.1.call-update) | async-done | bytes 4194320 | tf_op jit(solution)/shard_map/all_gather | solution.py:19
  124.4 23.2 %all-gather.16.cloned.1.call-done = bf16[4096,128]{1,0:T(8,128)(2,1)} async-done(((bf16[512,128]{1,0:T(8,128)(2,1)}), bf16[4096,128]{1,0:T(8,128)(2,1)}) %all-gather.16.cloned.1.call-update) | async-done | bytes 1048592 | tf_op jit(solution)/shard_map/all_gather | solution.py:64
  147.6 4.7 %fusion.6 = bf16[512,128]{0,1:T(8,128)(2,1)} fusion(bf16[4096,128]{1,0:T(8,128)(2,1)} %all-gather.16.cloned.1.call-done, bf16[512,4096]{1,0:T(8,128)(2,1)} %all-gather.18.cloned.1.call-done), kind=kOutput, calls=%fused_computation.14 | convolution fusion | flops 536936448 | bytes 5373952 | tf_op jit(solution)/shard_map/dot_general | solution.py:11
  152.3 0.0 all-gather.20.cloned.1.call-update
  152.3 0.0 all-gather.28.cloned.1.call-start
  152.4 0.7 all-gather.28.cloned.1.call-update
  153.1 0.0 all-gather.26.cloned.1.call-start
  153.1 31.9 %all-gather.24.cloned.1.call-done = bf16[512,2048]{1,0:T(8,128)(2,1)} async-done(((bf16[512,512]{1,0:T(8,128)(2,1)}), bf16[512,2048]{1,0:T(8,128)(2,1)}) %all-gather.24.cloned.1.call-update) | async-done | bytes 2097168 | tf_op jit(solution)/shard_map/all_gather | solution.py:44
  185.0 3.1 convolution_convert_fusion.1
  188.1 0.0 all-gather.26.cloned.1.call-update
  188.1 0.0 all-gather.30.cloned.1.call-start
  188.2 51.2 %all-gather.22.cloned.1.call-done = bf16[512,4096]{1,0:T(8,128)(2,1)} async-done(((bf16[512,1024]{1,0:T(8,128)(2,1)}), bf16[512,4096]{1,0:T(8,128)(2,1)}) %all-gather.22.cloned.1.call-update) | async-done | bytes 4194320 | tf_op jit(solution)/shard_map/all_gather | solution.py:19
  239.3 23.2 %all-gather.20.cloned.1.call-done = bf16[4096,128]{0,1:T(8,128)(2,1)} async-done(((bf16[512,128]{0,1:T(8,128)(2,1)}), bf16[4096,128]{0,1:T(8,128)(2,1)}) %all-gather.20.cloned.1.call-update) | async-done | bytes 1048592 | tf_op jit(solution)/shard_map/all_gather | solution.py:66
  262.5 4.7 %fusion.18 = (bf16[512,128]{0,1:T(8,128)(2,1)}, f32[512,128]{0,1:T(8,128)S(1)}) fusion(bf16[4096,128]{0,1:T(8,128)(2,1)} %all-gather.20.cloned.1.call-done, bf16[512,4096]{1,0:T(8,128)(2,1)} %all-gather.22.cloned.1.call-done), kind=kOutput, calls=%fused_computation.26 | convolution fusion | flops 536936448 | bytes 5636096 | tf_op jit(solution)/shard_map/dot_general | solution.py:11
  267.3 0.0 all-gather.32.cloned.1.call-start
  267.3 0.7 all-gather.32.cloned.1.call-update
  268.0 32.2 %all-gather.28.cloned.1.call-done = bf16[2,256,2048]{2,1,0:T(8,128)(2,1)} async-done(((bf16[2,256,512]{2,1,0:T(8,128)(2,1)}), bf16[2,256,2048]{2,1,0:T(8,128)(2,1)}) %all-gather.28.cloned.1.call-update) | async-done | bytes 2097168 | tf_op jit(solution)/shard_map/all_gather | solution.py:75
  300.3 25.1 %all-gather.26.cloned.1.call-done = bf16[2,2048,128]{1,2,0:T(8,128)(2,1)} async-done(((bf16[2,256,128]{1,2,0:T(8,128)(2,1)}), bf16[2,2048,128]{1,2,0:T(8,128)(2,1)}) %all-gather.26.cloned.1.call-update) | async-done | bytes 1048592 | tf_op jit(solution)/shard_map/all_gather | solution.py:70
  325.3 2.7 fusion.19
  328.1 0.8 copy.14
  328.9 19.2 %all-gather.30.cloned.1.call-done = bf16[4096,128]{0,1:T(8,128)(2,1)} async-done(((bf16[512,128]{0,1:T(8,128)(2,1)}), bf16[4096,128]{0,1:T(8,128)(2,1)}) %all-gather.30.cloned.1.call-update) | async-done | bytes 1048592 | tf_op jit(solution)/shard_map/all_gather | solution.py:71
  348.2 1.6 copy.12
  349.8 12.1 %gather_fusion = bf16[4096,128]{1,0:T(8,128)(2,1)S(1)} fusion(bf16[4096,128]{1,0:T(8,128)(2,1)S(1)} %copy.12, s32[4096]{0:T(1024)S(1)} %fusion.14), kind=kCustom, calls=%fused_computation | custom fusion | bytes 2113536 | tf_op jit(solution)/shard_map/jit(_take)/gather | solution.py:73
  361.9 0.5 copy.13
  362.5 23.5 %all-gather.32.cloned.1.call-done = bf16[2,256,2048]{2,1,0:T(8,128)(2,1)} async-done(((bf16[2,256,512]{2,1,0:T(8,128)(2,1)}), bf16[2,256,2048]{2,1,0:T(8,128)(2,1)}) %all-gather.32.cloned.1.call-update) | async-done | bytes 2097168 | tf_op jit(solution)/shard_map/all_gather | solution.py:76
  385.9 2.4 fusion.4
  388.3 0.8 copy.15
  (12 shorter events, 0.1 us)
Async XLA Ops:
  7.2 3.3 copy-start.2
  7.2 62.8 %copy-start.3 = (f32[512,128]{1,0:T(8,128)S(1)}, f32[512,128]{1,0:T(8,128)}, u32[]{:S(2)}) copy-start(f32[512,128]{1,0:T(8,128)} %param.11) | copy-start | bytes 786436
  7.2 25.0 %all-gather.12.cloned.1.call-start = ((), (), s32[]{:S(2)}) async-start(), calls=%async_computation.1 | async-start | bytes 1179648 | tf_op jit(solution)/shard_map/all_gather | solution.py:40
  8.9 61.0 %all-gather.14.cloned.1.call-start = ((), (), s32[]{:S(2)}) async-start(), calls=%async_computation.2 | async-start | bytes 2621440 | tf_op jit(solution)/shard_map/all_gather | solution.py:45
  9.7 114.7 %all-gather.18.cloned.1.call-start = ((), (), s32[]{:S(2)}) async-start(), calls=%async_computation.4 | async-start | bytes 5242880 | tf_op jit(solution)/shard_map/all_gather | solution.py:19
  10.4 137.2 %all-gather.16.cloned.1.call-start = ((), (), s32[]{:S(2)}) async-start(), calls=%async_computation.3 | async-start | bytes 1179648 | tf_op jit(solution)/shard_map/all_gather | solution.py:64
  73.7 29.2 %copy-start.1 = (f32[512,128]{1,0:T(8,128)S(1)}, f32[512,128]{1,0:T(8,128)}, u32[]{:S(2)}) copy-start(f32[512,128]{1,0:T(8,128)} %param.12) | copy-start | bytes 786436
  103.6 81.4 %all-gather.24.cloned.1.call-start = ((), (), s32[]{:S(2)}) async-start(), calls=%async_computation.7 | async-start | bytes 2621440 | tf_op jit(solution)/shard_map/all_gather | solution.py:44
  104.2 135.1 %all-gather.22.cloned.1.call-start = ((), (), s32[]{:S(2)}) async-start(), calls=%async_computation.6 | async-start | bytes 5242880 | tf_op jit(solution)/shard_map/all_gather | solution.py:19
  104.8 80.3 %copy-start = (bf16[2,2048,128]{2,1,0:T(8,128)(2,1)S(1)}, bf16[2,2048,128]{2,1,0:T(8,128)(2,1)}, u32[]{:S(2)}) copy-start(bf16[2,2048,128]{2,1,0:T(8,128)(2,1)} %all-gather.12.cloned.1.call-done) | copy-start | bytes 3145732
  104.8 157.8 %all-gather.20.cloned.1.call-start = ((), (), s32[]{:S(2)}) async-start(), calls=%async_computation.5 | async-start | bytes 1179648 | tf_op jit(solution)/shard_map/all_gather | solution.py:66
  152.3 147.9 %all-gather.28.cloned.1.call-start = ((), (), s32[]{:S(2)}) async-start(), calls=%async_computation.9 | async-start | bytes 2621440 | tf_op jit(solution)/shard_map/all_gather | solution.py:75
  153.1 172.3 %all-gather.26.cloned.1.call-start = ((), (), s32[]{:S(2)}) async-start(), calls=%async_computation.8 | async-start | bytes 1179648 | tf_op jit(solution)/shard_map/all_gather | solution.py:70
  188.1 160.0 %all-gather.30.cloned.1.call-start = ((), (), s32[]{:S(2)}) async-start(), calls=%async_computation.10 | async-start | bytes 1179648 | tf_op jit(solution)/shard_map/all_gather | solution.py:71
  267.3 118.7 %all-gather.32.cloned.1.call-start = ((), (), s32[]{:S(2)}) async-start(), calls=%async_computation.11 | async-start | bytes 2621440 | tf_op jit(solution)/shard_map/all_gather | solution.py:76
Sparse Core Ops, SparseCore 0:
  10.2 21.9 all-gather.11
  34.0 35.8 all-gather.13
  71.8 52.5 all-gather.17
  126.4 21.1 all-gather.15
  149.3 35.6 all-gather.23
  186.7 52.5 all-gather.21
  241.5 20.9 all-gather.19
  264.4 35.8 all-gather.27
  302.4 22.8 all-gather.25
  327.4 20.7 all-gather.29
  350.0 35.8 all-gather.31
where the time goes:
time: 398 us; the launch traced here: 396 us
  waiting for transfers between devices  312 us (78%)
  blocking collectives  29.1 us (7%)
  matrix products  21.4 us (5%)
  local copies, waits for them, and re-layouts  16 us (4%)
  between operations  14 us (4%)
    all_gather x2, waiting for transfers between devices, through(): return product(lax.all_gather(factor, 'rhs', axis=1, tiled=True), vector)  70.7 us
    all_gather x1, waiting for transfers between devices, shards(): lax.all_gather(lower_update, 'rhs', axis=1, tiled=True)  37.7 us
    all_gather x1, waiting for transfers between devices, shards(): lax.all_gather(upper_pivot, 'rhs', axis=2, tiled=True)  32.2 us
    all_gather x1, waiting for transfers between devices, shards(): lax.all_gather(lower_flat, 'rhs', axis=1, tiled=True)  31.9 us
    all_to_all x1, blocking collectives, shards(): lax.all_to_all(spread, 'panel', split_axis=0, concat_axis=0, tiled=True)  29.1 us
    all_gather x1, waiting for transfers between devices, shards(): lax.all_gather(pivot_half, 'panel', axis=1, tiled=True)  25.1 us
    all_gather x1, waiting for transfers between devices, shards(): lax.all_gather(upper_update, 'rhs', axis=2, tiled=True)  23.5 us
    all_gather x1, waiting for transfers between devices, shards(): lax.all_gather(parent_sum.astype(jnp.bfloat16), 'panel', axis=0, tiled=True)  23.2 us
  transfers between devices with their start and end apart: 11, of which 11 were waited for; matrix products, arithmetic and copies ran while one was open for 9% of the time, Pallas kernels for 0%

commit v1 on v0

v1 whole, which is shorter than its diff:
```python
import functools

import jax
import jax.numpy as jnp
from jax import lax
from jax.experimental import pallas as pl
from jax.experimental.pallas import tpu as pltpu
from jax.sharding import PartitionSpec as P

BF = jnp.bfloat16
F32 = jnp.float32
MESH = pl.DeviceIdType.MESH


def dot(left, right):
    return jnp.dot(left, right, preferred_element_type=F32)


def kernel(
    panels,
    cols,
    pivot_rhs,
    update_rhs,
    parent_rhs,
    lower_pivot,
    lower_update,
    parent_lower,
    parent_upper,
    upper_pivot,
    upper_update,
    row_map,
    col_map,
    parent_out,
    child_out,
    pin,
    phalf,
    vec,
    x_pin,
    x_half,
    x_par,
    s_up,
    r_up,
    s_piv,
    r_piv,
    s_par,
    r_par,
    s_ch,
    r_ch,
    uhalf,
    moved,
    picked,
    direct,
    g_send,
    g_recv,
    f_send,
    rs_send,
    rs_recv,
    sh_send,
    sh_recv,
):
    me_p, me_r = lax.axis_index("panel"), lax.axis_index("rhs")
    total = panels * cols
    me = me_p * cols + me_r
    core = lax.rem(me_p, 2)
    mate = me_p + 1 - 2 * core
    per = panels // cols
    half = panels // 2
    m = parent_rhs.shape[0]
    mk = pivot_rhs.shape[1]
    child = me_p // half

    barrier = pltpu.get_barrier_semaphore()

    @pl.loop(1, total)
    def _(step):
        other = lax.rem(me + step, total)
        pl.semaphore_signal(
            barrier,
            inc=1,
            device_id=(other // cols, lax.rem(other, cols)),
            device_id_type=MESH,
        )

    pin[...] = pivot_rhs[...].astype(BF)
    pl.semaphore_wait(barrier, total - 1)

    def spot(buffer, depth, column, part):
        return buffer.at[column, :, pl.ds(pl.multiple_of(part * depth, depth), depth), :]

    def send_copy(stage, block, buffer, depth, step):
        goal = lax.rem(me_p // 2 + step, half) * 2 + core
        return pltpu.make_async_remote_copy(
            src_ref=block,
            dst_ref=spot(buffer, depth, me_r, lax.rem(me_p, per)),
            send_sem=g_send.at[stage, step],
            recv_sem=g_recv.at[stage, me_r, lax.rem(me_p, per)],
            device_id=(goal, me_p // per),
            device_id_type=MESH,
        )

    def gather_start(stage, block, buffer, depth):
        for step in list(range(1, half)):
            send_copy(stage, block, buffer, depth, step).start()
        own = me_p // per == me_r

        @pl.when(own)
        def _():
            pltpu.make_async_copy(
                block,
                spot(buffer, depth, me_r, lax.rem(me_p, per)),
                g_recv.at[stage, me_r, lax.rem(me_p, per)],
            ).start()

        @pl.when(jnp.logical_not(own))
        def _():
            send_copy(stage, block, buffer, depth, 0).start()

    def gather_end(stage, block, buffer, depth):
        for step in range(1, half):
            send_copy(stage, block, buffer, depth, step).wait_send()

        @pl.when(me_p // per != me_r)
        def _():
            send_copy(stage, block, buffer, depth, 0).wait_send()

        for step in range(cols):
            for pair in range(per // 2):
                forward(stage, buffer, depth, step, pair).wait_send()

    def forward(stage, buffer, depth, step, pair):
        column = lax.rem(me_r + 1 + step, cols)
        part = 2 * pair + core
        place = spot(buffer, depth, column, part)
        return pltpu.make_async_remote_copy(
            src_ref=place,
            dst_ref=place,
            send_sem=f_send.at[stage, step, pair],
            recv_sem=g_recv.at[stage, column, part],
            device_id=(mate, me_r),
            device_id_type=MESH,
        )

    def landed(stage, buffer, depth, column, part):
        place = spot(buffer, depth, column, part)
        pltpu.make_async_copy(place, place, g_recv.at[stage, column, part]).wait()

    def pass_on(stage, buffer, depth):
        for step in range(cols):
            for pair in range(per // 2):
                column = lax.rem(me_r + 1 + step, cols)
                landed(stage, buffer, depth, column, 2 * pair + core)
                forward(stage, buffer, depth, step, pair).start()

    def arrive(stage, buffer, depth, step):
        column = lax.rem(me_r + 1 + step, cols)
        for pair in range(per // 2):
            landed(stage, buffer, depth, column, 2 * pair + 1 - core)
        return column

    def scatter_copy(stage, source, target, step):
        return pltpu.make_async_remote_copy(
            src_ref=source.at[step],
            dst_ref=target.at[step],
            send_sem=rs_send.at[stage, step],
            recv_sem=rs_recv.at[stage, step],
            device_id=(me_p, lax.rem(me_r + 1 + step, cols)),
            device_id_type=MESH,
        )

    def scatter_sum(stage, source, target, value):
        for step in range(cols - 1):
            scatter_copy(stage, source, target, step).wait_recv()
            value = value + target[step].astype(F32)
        for step in range(cols - 1):
            scatter_copy(stage, source, target, step).wait_send()
        return value

    last = cols - 1

    gather_start(0, pin, x_pin, mk)

    width = upper_update.shape[2]
    for k in range(2):
        rows = lax.broadcasted_iota(jnp.int32, (per * m, width), 0)
        chosen = (rows == col_map[k : k + 1, :]).astype(F32).astype(BF)
        picked[k] = lax.dot_general(
            upper_update[k], chosen, (((1,), (1,)), ((), ())), preferred_element_type=F32
        ).astype(BF)

    pass_on(0, x_pin, mk)
    update = update_rhs[...]
    for step in range(cols):
        column = arrive(0, x_pin, mk, step)
        value = dot(lower_update[...], x_pin[column, child])
        if step < last:
            s_up[step] = value.astype(BF)
            scatter_copy(0, s_up, r_up, step).start()
        else:
            update = update + value
    for step in range(cols):
        column = lax.rem(me_r + 1 + step, cols)
        for k in range(2):
            value = dot(lower_pivot[k], x_pin[column, k])
            if step < last:
                s_piv[step, k] = value.astype(BF)
            else:
                direct[step, k] = value
        if step < last:
            scatter_copy(1, s_piv, r_piv, step).start()
    gather_end(0, pin, x_pin, mk)
    update = scatter_sum(0, s_up, r_up, update).astype(BF)
    uhalf[0] = update[: m // 2]
    uhalf[1] = update[m // 2 :]
    first = lax.rem(me_p, half) * 2

    def shuffle(side):
        return pltpu.make_async_remote_copy(
            src_ref=uhalf.at[side],
            dst_ref=moved.at[child],
            send_sem=sh_send.at[side],
            recv_sem=sh_recv.at[child],
            device_id=(first + side, me_r),
            device_id_type=MESH,
        )

    for side in range(2):

        @pl.when(first + side != me_p)
        def _():
            shuffle(side).start()

        @pl.when(first + side == me_p)
        def _():
            pltpu.make_async_copy(uhalf.at[side], moved.at[child], sh_recv.at[child]).start()

    phalf[...] = scatter_sum(1, s_piv, r_piv, direct[last]).astype(BF)
    rows = lax.broadcasted_iota(jnp.int32, (m, m // 2), 0)
    spread = parent_rhs[...]
    for k in range(2):
        pltpu.make_async_copy(moved.at[k], moved.at[k], sh_recv.at[k]).wait()
        chosen = (rows == row_map[k : k + 1, :]).astype(F32).astype(BF)
        spread = spread + dot(chosen, moved[k])
    vec[0, 0] = spread.astype(BF)
    for side in range(2):

        @pl.when(first + side != me_p)
        def _():
            shuffle(side).wait_send()

    gather_start(1, vec.at[0], x_par.at[0], m)
    gather_start(2, phalf, x_half, mk)

    for level, factor in ((0, parent_lower), (1, parent_upper)):
        stage = 1 if level == 0 else 3
        block, buffer = vec.at[level], x_par.at[level]
        pass_on(stage, buffer, m)
        value = None
        for step in range(cols):
            column = arrive(stage, buffer, m, step)
            value = dot(factor[...], x_par[level, column, 0])
            if step < last:
                s_par[level, step] = value.astype(BF)
                scatter_copy(2 + level, s_par.at[level], r_par.at[level], step).start()
        gather_end(stage, block, buffer, m)
        value = scatter_sum(2 + level, s_par.at[level], r_par.at[level], value)
        vec[level + 1, 0] = value.astype(BF)
        following = 3 if level == 0 else 4
        gather_start(following, vec.at[level + 1], x_par.at[level + 1], m)
        if level == 0:
            pass_on(2, x_half, mk)
            for step in range(cols):
                column = arrive(2, x_half, mk, step)
                for k in range(2):
                    direct[step, k] = dot(upper_pivot[k], x_half[column, k])
            gather_end(2, phalf, x_half, mk)
        else:
            parent_out[...] = value

    pass_on(4, x_par.at[2], m)
    for step in range(cols):
        column = arrive(4, x_par.at[2], m, step)
        for k in range(2):
            value = direct[step, k] + dot(picked[k], x_par[2, column, 0])
            if step < last:
                s_ch[step, k] = value.astype(BF)
            else:
                direct[step, k] = value
        if step < last:
            scatter_copy(4, s_ch, r_ch, step).start()
    gather_end(4, vec.at[2], x_par.at[2], m)
    child_out[...] = scatter_sum(4, s_ch, r_ch, direct[last])


def shards(panels, cols, *arguments):
    *arrays, maps = arguments
    m, width = arrays[1].shape
    mk = arrays[0].shape[1]
    per = panels // cols
    sides = maps.reshape(2, -1)
    me_p, me_r = lax.axis_index("panel"), lax.axis_index("rhs")
    row_map = lax.dynamic_slice_in_dim(sides, me_p * (m // 2), m // 2, 1) - me_p * m
    wide = arrays[8].shape[2]
    col_map = lax.dynamic_slice_in_dim(sides, me_r * wide, wide, 1) - me_r * per * m
    vm = pltpu.VMEM
    dma = pltpu.SemaphoreType.DMA
    return pl.pallas_call(
        functools.partial(kernel, panels, cols),
        out_shape=(
            jax.ShapeDtypeStruct((m, width), F32),
            jax.ShapeDtypeStruct((2, mk, width), F32),
        ),
        in_specs=[pl.BlockSpec(memory_space=pltpu.VMEM)] * 11,
        out_specs=(pl.BlockSpec(memory_space=pltpu.VMEM),) * 2,
        scratch_shapes=[
            vm((2, mk, width), BF),
            vm((2, mk, width), BF),
            vm((3, 1, m, width), BF),
            vm((cols, 2, per * mk, width), BF),
            vm((cols, 2, per * mk, width), BF),
            vm((3, cols, 1, per * m, width), BF),
            vm((cols - 1, m, width), BF),
            vm((cols - 1, m, width), BF),
            vm((cols - 1, 2, mk, width), BF),
            vm((cols - 1, 2, mk, width), BF),
            vm((2, cols - 1, m, width), BF),
            vm((2, cols - 1, m, width), BF),
            vm((cols - 1, 2, mk, width), BF),
            vm((cols - 1, 2, mk, width), BF),
            vm((2, m // 2, width), BF),
            vm((2, m // 2, width), BF),
            vm((2, mk, per * m), BF),
            vm((cols, 2, mk, width), F32),
            dma((5, panels // 2)),
            dma((5, cols, per)),
            dma((5, cols, per // 2)),
            dma((5, cols - 1)),
            dma((5, cols - 1)),
            dma((2,)),
            dma((2,)),
        ],
        compiler_params=pltpu.CompilerParams(
            collective_id=0, has_side_effects=True, vmem_limit_bytes=60 * 1024 * 1024
        ),
    )(*arrays, row_map, col_map)


def solution(mesh):
    panels, cols = mesh.shape["panel"], mesh.shape["rhs"]
    placed = (
        P(None, "panel", "rhs"),
        P("panel", "rhs"),
        P("panel", "rhs"),
        P(None, "panel", "rhs"),
        P("panel", "rhs"),
        P("panel", "rhs"),
        P("panel", "rhs"),
        P(None, "panel", "rhs"),
        P(None, "panel", "rhs"),
        P(),
    )
    return jax.shard_map(
        functools.partial(shards, panels, cols),
        mesh=mesh,
        in_specs=placed,
        out_specs=(P("panel", "rhs"), P(None, "panel", "rhs")),
        check_vma=False,
    )
```

time: 398 us -> 126 us (0.32)
  waiting for transfers between devices: 312 us -> 0 us
  Pallas kernels: 0 us -> 120 us
  blocking collectives: 29.1 us -> 0 us
  matrix products: 21.4 us -> 0 us
  between operations: 14 us -> 0.66 us
  local copies, waits for them, and re-layouts: 16 us -> 3.13 us
    all_gather x11 -> x0, waiting for transfers between devices: 308 us -> none  [the longest x2 70.7 us: through(): return product(lax.all_gather(factor, 'rhs', axis=1, tiled=True), vector)]
    pallas_call x0 -> x1, Pallas kernels: none -> 120 us  [shards(): pl.pallas_call(functools.partial(kernel, panels, cols), out_shape=(jax.Sh...]
    all_to_all x1 -> x0, blocking collectives: 29.1 us -> none  [shards(): lax.all_to_all(spread, 'panel', split_axis=0, concat_axis=0, tiled=True)]
    dot_general x6 -> x0, matrix products: 21.4 us -> none  [the longest x3 13.1 us: product(): return jnp.dot(left, right, preferred_element_type=jnp.float32)]
    gather x2 -> x0, local copies, waits for them, and re-layouts: 12.7 us -> none  [shards(): remote_rows = jnp.take(solution_all, maps, axis=0).reshape(2, FU, rhs_width)]
  transfers between devices with their start and end apart: 11 -> 0, of which waited for: 11 -> 0; matrix products, arithmetic and copies ran while one was open for 9% -> 0% of each run, Pallas kernels for 0% -> 0%
where the time goes in v1:
time: 126 us; the launch traced here: 125 us
  Pallas kernels  120 us (95%)
  local copies, waits for them, and re-layouts  3.13 us (2%)
    pallas_call x1, Pallas kernels, shards(): pl.pallas_call(functools.partial(kernel, panels, cols), out_shape=(jax.Sh...  120 us
    unnamed x6, local copies, waits for them, and re-layouts  3.12 us

profile of v1, /device:TPU:24, one launch (start us, length us, event | category | flops | bytes accessed | tf_op | source)
XLA Modules:
  0.0 125.2 jit_solution(2539262199052332128)
XLA Ops:
  0.6 0.0 copy-start.1
  0.6 0.7 copy-done.1
  1.4 0.6 dynamic-slice_subtract_fusion.1.row_map
  1.9 0.6 dynamic-slice_subtract_fusion.col_map
  2.5 120.2 %shard_map.113 = (f32[512,128]{1,0:T(8,128)}, f32[2,256,128]{2,1,0:T(8,128)}) custom-call(f32[2,256,128]{2,1,0:T(8,128)} %pivot_rhs.1, f32[512,128]{1,0:T(8,128)} %update_rhs.1, f32[512,128]{1,0:T(8,128)} %parent_rhs.1, bf16[2,256,512]{2,1,0:T(8,128)(2,1)} %lower_pivot.1, bf16[512,512]{1,0:T(8,128)(2,1)} %lower_update.1, bf16[512,1024]{1,0:T(8,128)(2,1)} %parent_lower.1, ...), custom_call_target="tpu_custom_call" | custom-call | tf_op jit(solution)/shard_map/pallas_call | solution.py:306
  122.7 0.0 copy-start
  122.8 1.7 %copy.14 = f32[512,128]{1,0:T(8,128)} copy(f32[512,128]{1,0:T(8,128)} %get-tuple-element.4) | data formatting | bytes 524288
  124.5 0.0 copy-done
  124.5 0.7 copy.15
  (1 shorter events, 0.0 us)
Async XLA Ops:
  0.6 0.7 copy-start.1
  122.7 1.7 %copy-start = (f32[2,256,128]{2,1,0:T(8,128)S(1)}, f32[2,256,128]{2,1,0:T(8,128)}, u32[]{:S(2)}) copy-start(f32[2,256,128]{2,1,0:T(8,128)} %get-tuple-element.5) | copy-start | bytes 786436

commit v2 on v1

v2 whole, which is shorter than its diff:
```python
import functools

import jax
import jax.numpy as jnp
from jax import lax
from jax.experimental import pallas as pl
from jax.experimental.pallas import tpu as pltpu
from jax.sharding import PartitionSpec as P

BF = jnp.bfloat16
F32 = jnp.float32
MESH = pl.DeviceIdType.MESH


def dot(left, right):
    return jnp.dot(left, right, preferred_element_type=F32)


def kernel(
    panels,
    cols,
    pivot_rhs,
    update_rhs,
    parent_rhs,
    lower_pivot,
    lower_update,
    parent_lower,
    parent_upper,
    upper_pivot,
    upper_update,
    row_map,
    col_map,
    parent_out,
    child_out,
    pin,
    phalf,
    vec,
    x_pin,
    x_half,
    x_par,
    s_up,
    r_up,
    s_piv,
    r_piv,
    s_par,
    r_par,
    s_ch,
    r_ch,
    uhalf,
    moved,
    picked,
    direct,
    par_sum,
    spread_sum,
    child_sum,
    g_send,
    g_recv,
    f_send,
    rs_send,
    rs_recv,
    sh_send,
    sh_recv,
):
    me_p, me_r = lax.axis_index("panel"), lax.axis_index("rhs")
    total = panels * cols
    me = me_p * cols + me_r
    core = lax.rem(me_p, 2)
    mate = me_p + 1 - 2 * core
    per = panels // cols
    half = panels // 2
    m = parent_rhs.shape[0]
    mk = pivot_rhs.shape[1]
    child = me_p // half

    barrier = pltpu.get_barrier_semaphore()

    @pl.loop(1, total)
    def _(step):
        other = lax.rem(me + step, total)
        pl.semaphore_signal(
            barrier,
            inc=1,
            device_id=(other // cols, lax.rem(other, cols)),
            device_id_type=MESH,
        )

    pin[...] = pivot_rhs[...].astype(BF)
    direct[...] = jnp.zeros_like(direct)
    pl.semaphore_wait(barrier, total - 1)

    group = me_p // per
    last = cols - 1

    def every(source, goal):
        return None

    def below(source, goal):
        return goal >= source

    def above(source, goal):
        return goal <= source

    def guard(condition, action):
        if condition is None:
            action()
        else:
            pl.when(condition)(action)

    def both(first, second):
        return second if first is None else jnp.logical_and(first, second)

    def spot(buffer, depth, column, part, lead):
        rows = pl.ds(pl.multiple_of(part * depth, depth), depth)
        return buffer.at[column, slice(None) if lead is None else pl.ds(lead, 1), rows, :]

    class Gather:
        def __init__(self, stage, block, buffer, depth, keep, lead):
            self.stage, self.block, self.buffer, self.depth = stage, block, buffer, depth
            self.keep, self.lead = keep, lead
            self.active = keep(me_r, group)

        def place(self, column, part, panel):
            return spot(self.buffer, self.depth, column, part, self.lead(panel))

        def piece(self, panel):
            lead = self.lead(panel)
            return self.block if lead is None else self.block.at[pl.ds(lead, 1)]

        def goal(self, step):
            return lax.rem(me_p // 2 + step, half) * 2 + core

        def copy(self, step):
            goal = self.goal(step)
            return pltpu.make_async_remote_copy(
                src_ref=self.piece(goal),
                dst_ref=self.place(me_r, lax.rem(me_p, per), goal),
                send_sem=g_send.at[self.stage, step],
                recv_sem=g_recv.at[self.stage, me_r, lax.rem(me_p, per)],
                device_id=(goal, group),
                device_id_type=MESH,
            )

        def sends(self, action):
            for step in list(range(1, half)) + [0]:
                condition = self.keep(group, self.goal(step) // per)
                if step == 0:
                    condition = both(condition, group != me_r)
                guard(condition, functools.partial(action, step))

        def start(self):
            self.sends(lambda step: self.copy(step).start())

            @pl.when(group == me_r)
            def _():
                part = lax.rem(me_p, per)
                pltpu.make_async_copy(
                    self.piece(me_p),
                    self.place(me_r, part, me_p),
                    g_recv.at[self.stage, me_r, part],
                ).start()

        def landed(self, column, part):
            place = self.place(column, part, me_p)
            pltpu.make_async_copy(place, place, g_recv.at[self.stage, column, part]).wait()

        def forward(self, step, pair):
            column = lax.rem(me_r + 1 + step, cols)
            part = 2 * pair + core
            return pltpu.make_async_remote_copy(
                src_ref=self.place(column, part, me_p),
                dst_ref=self.place(column, part, me_p),
                send_sem=f_send.at[self.stage, step, pair],
                recv_sem=g_recv.at[self.stage, column, part],
                device_id=(mate, me_r),
                device_id_type=MESH,
            )

        def pass_on(self):
            def action():
                for step in range(cols):
                    for pair in range(per // 2):
                        self.landed(lax.rem(me_r + 1 + step, cols), 2 * pair + core)
                        self.forward(step, pair).start()

            guard(self.active, action)

        def arrive(self, step):
            column = lax.rem(me_r + 1 + step, cols)
            for pair in range(per // 2):
                self.landed(column, 2 * pair + 1 - core)
            return column

        def finish(self):
            self.sends(lambda step: self.copy(step).wait_send())

            def action():
                for step in range(cols):
                    for pair in range(per // 2):
                        self.forward(step, pair).wait_send()

            guard(self.active, action)

    class Scatter:
        def __init__(self, stage, source, target, keep):
            self.stage, self.source, self.target, self.keep = stage, source, target, keep
            self.active = keep(me_r, group)

        def copy(self, step):
            return pltpu.make_async_remote_copy(
                src_ref=self.source.at[step],
                dst_ref=self.target.at[step],
                send_sem=rs_send.at[self.stage, step],
                recv_sem=rs_recv.at[self.stage, step],
                device_id=(me_p, lax.rem(me_r + 1 + step, cols)),
                device_id_type=MESH,
            )

        def add(self, total_ref):
            for step in range(last):
                sender = lax.rem(me_r + last - step, cols)

                def action(step=step):
                    self.copy(step).wait_recv()
                    total_ref[...] += self.target[step].astype(F32)

                guard(self.keep(sender, group), action)

        def finish(self):
            def action():
                for step in range(last):
                    self.copy(step).wait_send()

            guard(self.active, action)

    def whole(panel):
        return None

    def same(panel):
        return panel // half

    def other(panel):
        return 1 - panel // half

    g_own = Gather(0, pin, x_pin, mk, every, same)
    g_other = Gather(5, pin, x_pin, mk, below, other)
    g_low = Gather(1, vec.at[0], x_par.at[0], m, below, whole)
    g_half = Gather(2, phalf, x_half, mk, above, whole)
    g_up = Gather(3, vec.at[1], x_par.at[1], m, above, whole)
    g_all = Gather(4, vec.at[2], x_par.at[2], m, every, whole)
    t_up = Scatter(0, s_up, r_up, every)
    t_piv = Scatter(1, s_piv, r_piv, below)
    t_low = Scatter(2, s_par.at[0], r_par.at[0], below)
    t_high = Scatter(3, s_par.at[1], r_par.at[1], above)
    t_child = Scatter(4, s_ch, r_ch, every)

    g_own.start()
    g_other.start()

    width = upper_update.shape[2]
    for k in range(2):
        rows = lax.broadcasted_iota(jnp.int32, (per * m, width), 0)
        chosen = (rows == col_map[k : k + 1, :]).astype(F32).astype(BF)
        picked[k] = lax.dot_general(
            upper_update[k], chosen, (((1,), (1,)), ((), ())), preferred_element_type=F32
        ).astype(BF)
    spread_sum[...] = parent_rhs[...]

    g_own.pass_on()
    for step in range(cols):
        column = g_own.arrive(step)
        value = dot(lower_update[...], x_pin[column, child])
        if step < last:
            s_up[step] = value.astype(BF)
            t_up.copy(step).start()
        else:
            par_sum[...] = update_rhs[...] + value
    g_other.pass_on()
    t_up.add(par_sum)
    update = par_sum[...].astype(BF)
    uhalf[0] = update[: m // 2]
    uhalf[1] = update[m // 2 :]
    first = lax.rem(me_p, half) * 2

    def shuffle(side):
        return pltpu.make_async_remote_copy(
            src_ref=uhalf.at[side],
            dst_ref=moved.at[child],
            send_sem=sh_send.at[side],
            recv_sem=sh_recv.at[child],
            device_id=(first + side, me_r),
            device_id_type=MESH,
        )

    for side in range(2):

        @pl.when(first + side != me_p)
        def _():
            shuffle(side).start()

        @pl.when(first + side == me_p)
        def _():
            pltpu.make_async_copy(uhalf.at[side], moved.at[child], sh_recv.at[child]).start()

    child_sum[...] = jnp.zeros_like(child_sum)

    def pivots():
        for step in range(cols):
            column = g_other.arrive(step)
            for k in range(2):
                value = dot(lower_pivot[k], x_pin[column, k])
                if step < last:
                    s_piv[step, k] = value.astype(BF)
                else:
                    child_sum[k] = value
            if step < last:
                t_piv.copy(step).start()

    guard(g_other.active, pivots)

    rows = lax.broadcasted_iota(jnp.int32, (m, m // 2), 0)
    for k in range(2):
        pltpu.make_async_copy(moved.at[k], moved.at[k], sh_recv.at[k]).wait()
        chosen = (rows == row_map[k : k + 1, :]).astype(F32).astype(BF)
        spread_sum[...] += dot(chosen, moved[k])
    vec[0, 0] = spread_sum[...].astype(BF)
    g_low.start()

    t_piv.add(child_sum)
    phalf[...] = child_sum[...].astype(BF)
    g_half.start()

    def parent(level, gather, scatter, factor):
        par_sum[...] = jnp.zeros_like(par_sum)
        gather.pass_on()

        def action():
            for step in range(cols):
                column = gather.arrive(step)
                value = dot(factor[...], x_par[level, column, 0])
                if step < last:
                    s_par[level, step] = value.astype(BF)
                    scatter.copy(step).start()
                else:
                    par_sum[...] = value

        guard(gather.active, action)
        scatter.add(par_sum)
        vec[level + 1, 0] = par_sum[...].astype(BF)

    parent(0, g_low, t_low, parent_lower)
    g_up.start()
    g_half.pass_on()

    def known():
        for step in range(cols):
            column = g_half.arrive(step)
            for k in range(2):
                direct[step, k] = dot(upper_pivot[k], x_half[column, k])

    guard(g_half.active, known)
    parent(1, g_up, t_high, parent_upper)
    g_all.start()
    parent_out[...] = par_sum[...]

    g_all.pass_on()
    for step in range(cols):
        column = g_all.arrive(step)
        for k in range(2):
            value = direct[step, k] + dot(picked[k], x_par[2, column, 0])
            if step < last:
                s_ch[step, k] = value.astype(BF)
            else:
                child_out[k] = value
        if step < last:
            t_child.copy(step).start()
    for gather in (g_own, g_other, g_low, g_half, g_up, g_all):
        gather.finish()
    for side in range(2):

        @pl.when(first + side != me_p)
        def _():
            shuffle(side).wait_send()

    t_child.add(child_out)
    for scatter in (t_up, t_piv, t_low, t_high, t_child):
        scatter.finish()


def shards(panels, cols, *arguments):
    *arrays, maps = arguments
    m, width = arrays[1].shape
    mk = arrays[0].shape[1]
    per = panels // cols
    sides = maps.reshape(2, -1)
    me_p, me_r = lax.axis_index("panel"), lax.axis_index("rhs")
    row_map = lax.dynamic_slice_in_dim(sides, me_p * (m // 2), m // 2, 1) - me_p * m
    wide = arrays[8].shape[2]
    col_map = lax.dynamic_slice_in_dim(sides, me_r * wide, wide, 1) - me_r * per * m
    vm = pltpu.VMEM
    dma = pltpu.SemaphoreType.DMA
    return pl.pallas_call(
        functools.partial(kernel, panels, cols),
        out_shape=(
            jax.ShapeDtypeStruct((m, width), F32),
            jax.ShapeDtypeStruct((2, mk, width), F32),
        ),
        in_specs=[pl.BlockSpec(memory_space=pltpu.VMEM)] * 11,
        out_specs=(pl.BlockSpec(memory_space=pltpu.VMEM),) * 2,
        scratch_shapes=[
            vm((2, mk, width), BF),
            vm((2, mk, width), BF),
            vm((3, 1, m, width), BF),
            vm((cols, 2, per * mk, width), BF),
            vm((cols, 2, per * mk, width), BF),
            vm((3, cols, 1, per * m, width), BF),
            vm((cols - 1, m, width), BF),
            vm((cols - 1, m, width), BF),
            vm((cols - 1, 2, mk, width), BF),
            vm((cols - 1, 2, mk, width), BF),
            vm((2, cols - 1, m, width), BF),
            vm((2, cols - 1, m, width), BF),
            vm((cols - 1, 2, mk, width), BF),
            vm((cols - 1, 2, mk, width), BF),
            vm((2, m // 2, width), BF),
            vm((2, m // 2, width), BF),
            vm((2, mk, per * m), BF),
            vm((cols, 2, mk, width), F32),
            vm((m, width), F32),
            vm((m, width), F32),
            vm((2, mk, width), F32),
            dma((6, panels // 2)),
            dma((6, cols, per)),
            dma((6, cols, per // 2)),
            dma((5, cols - 1)),
            dma((5, cols - 1)),
            dma((2,)),
            dma((2,)),
        ],
        compiler_params=pltpu.CompilerParams(
            collective_id=0, has_side_effects=True, vmem_limit_bytes=60 * 1024 * 1024
        ),
    )(*arrays, row_map, col_map)


def solution(mesh):
    panels, cols = mesh.shape["panel"], mesh.shape["rhs"]
    placed = (
        P(None, "panel", "rhs"),
        P("panel", "rhs"),
        P("panel", "rhs"),
        P(None, "panel", "rhs"),
        P("panel", "rhs"),
        P("panel", "rhs"),
        P("panel", "rhs"),
        P(None, "panel", "rhs"),
        P(None, "panel", "rhs"),
        P(),
    )
    return jax.shard_map(
        functools.partial(shards, panels, cols),
        mesh=mesh,
        in_specs=placed,
        out_specs=(P("panel", "rhs"), P(None, "panel", "rhs")),
        check_vma=False,
    )
```

time: 126 us -> 109 us (0.87)
  Pallas kernels: 120 us -> 103 us
    pallas_call x1, Pallas kernels: 120 us -> 103 us  [shards(): pl.pallas_call(functools.partial(kernel, panels, cols), out_shape=(jax.Sh...]
where the time goes in v2:
time: 109 us; the launch traced here: 108 us
  Pallas kernels  103 us (94%)
  local copies, waits for them, and re-layouts  3.13 us (3%)
  other arithmetic  1.18 us (1%)
    pallas_call x1, Pallas kernels, shards(): pl.pallas_call(functools.partial(kernel, panels, cols), out_shape=(jax.Sh...  103 us
    unnamed x6, local copies, waits for them, and re-layouts  3.12 us

profile of v2, /device:TPU:24, one launch (start us, length us, event | category | flops | bytes accessed | tf_op | source)
XLA Modules:
  0.0 108.4 jit_solution(13360567849588053031)
XLA Ops:
  0.6 0.0 copy-start.1
  0.6 0.7 copy-done.1
  1.4 0.6 dynamic-slice_subtract_fusion.1.row_map
  1.9 0.6 dynamic-slice_subtract_fusion.col_map
  2.5 103.4 %shard_map.113 = (f32[512,128]{1,0:T(8,128)}, f32[2,256,128]{2,1,0:T(8,128)}) custom-call(f32[2,256,128]{2,1,0:T(8,128)} %pivot_rhs.1, f32[512,128]{1,0:T(8,128)} %update_rhs.1, f32[512,128]{1,0:T(8,128)} %parent_rhs.1, bf16[2,256,512]{2,1,0:T(8,128)(2,1)} %lower_pivot.1, bf16[512,512]{1,0:T(8,128)(2,1)} %lower_update.1, bf16[512,1024]{1,0:T(8,128)(2,1)} %parent_lower.1, ...), custom_call_target="tpu_custom_call" | custom-call | tf_op jit(solution)/shard_map/pallas_call | solution.py:401
  105.9 0.0 copy-start
  106.0 1.7 %copy.14 = f32[512,128]{1,0:T(8,128)} copy(f32[512,128]{1,0:T(8,128)} %get-tuple-element.4) | data formatting | bytes 524288
  107.7 0.0 copy-done
  107.7 0.7 copy.15
  (1 shorter events, 0.0 us)
Async XLA Ops:
  0.6 0.7 copy-start.1
  105.9 1.7 %copy-start = (f32[2,256,128]{2,1,0:T(8,128)S(1)}, f32[2,256,128]{2,1,0:T(8,128)}, u32[]{:S(2)}) copy-start(f32[2,256,128]{2,1,0:T(8,128)} %get-tuple-element.5) | copy-start | bytes 786436

commit v3 on v2

--- a/solution.py
+++ b/solution.py
@@ -115,27 +115,29 @@
 
     class Gather:
         def __init__(self, stage, block, buffer, depth, keep, lead):
-            self.stage, self.block, self.buffer, self.depth = stage, block, buffer, depth
+            self.stage, self.block, self.buffer, self.depth = stage, block, buffer, depth // 2
             self.keep, self.lead = keep, lead
             self.active = keep(me_r, group)
 
         def place(self, column, part, panel):
             return spot(self.buffer, self.depth, column, part, self.lead(panel))
 
-        def piece(self, panel):
+        def piece(self, panel, sub):
             lead = self.lead(panel)
-            return self.block if lead is None else self.block.at[pl.ds(lead, 1)]
+            rows = pl.ds(sub * self.depth, self.depth)
+            return self.block.at[slice(None) if lead is None else pl.ds(lead, 1), rows, :]
 
         def goal(self, step):
             return lax.rem(me_p // 2 + step, half) * 2 + core
 
-        def copy(self, step):
+        def copy(self, step, sub):
             goal = self.goal(step)
+            part = 2 * lax.rem(me_p, per) + sub
             return pltpu.make_async_remote_copy(
-                src_ref=self.piece(goal),
-                dst_ref=self.place(me_r, lax.rem(me_p, per), goal),
-                send_sem=g_send.at[self.stage, step],
-                recv_sem=g_recv.at[self.stage, me_r, lax.rem(me_p, per)],
+                src_ref=self.piece(goal, sub),
+                dst_ref=self.place(me_r, part, goal),
+                send_sem=g_send.at[self.stage, step, sub],
+                recv_sem=g_recv.at[self.stage, me_r, part],
                 device_id=(goal, group),
                 device_id_type=MESH,
             )
@@ -148,28 +150,33 @@
                 guard(condition, functools.partial(action, step))
 
         def start(self):
-            self.sends(lambda step: self.copy(step).start())
+            def action(step):
+                for sub in range(2):
+                    self.copy(step, sub).start()
+
+            self.sends(action)
 
             @pl.when(group == me_r)
             def _():
-                part = lax.rem(me_p, per)
-                pltpu.make_async_copy(
-                    self.piece(me_p),
-                    self.place(me_r, part, me_p),
-                    g_recv.at[self.stage, me_r, part],
-                ).start()
+                for sub in range(2):
+                    part = 2 * lax.rem(me_p, per) + sub
+                    pltpu.make_async_copy(
+                        self.piece(me_p, sub),
+                        self.place(me_r, part, me_p),
+                        g_recv.at[self.stage, me_r, part],
+                    ).start()
 
         def landed(self, column, part):
             place = self.place(column, part, me_p)
             pltpu.make_async_copy(place, place, g_recv.at[self.stage, column, part]).wait()
 
-        def forward(self, step, pair):
+        def forward(self, step, pair, sub):
             column = lax.rem(me_r + 1 + step, cols)
-            part = 2 * pair + core
+            part = 4 * pair + 2 * core + sub
             return pltpu.make_async_remote_copy(
                 src_ref=self.place(column, part, me_p),
                 dst_ref=self.place(column, part, me_p),
-                send_sem=f_send.at[self.stage, step, pair],
+                send_sem=f_send.at[self.stage, step, 2 * pair + sub],
                 recv_sem=g_recv.at[self.stage, column, part],
                 device_id=(mate, me_r),
                 device_id_type=MESH,
@@ -177,26 +184,34 @@
 
         def pass_on(self):
             def action():
-                for step in range(cols):
-                    for pair in range(per // 2):
-                        self.landed(lax.rem(me_r + 1 + step, cols), 2 * pair + core)
-                        self.forward(step, pair).start()
+                for sub in range(2):
+                    for step in range(cols):
+                        for pair in range(per // 2):
+                            column = lax.rem(me_r + 1 + step, cols)
+                            self.landed(column, 4 * pair + 2 * core + sub)
+                            self.forward(step, pair, sub).start()
 
             guard(self.active, action)
 
         def arrive(self, step):
             column = lax.rem(me_r + 1 + step, cols)
             for pair in range(per // 2):
-                self.landed(column, 2 * pair + 1 - core)
+                for sub in range(2):
+                    self.landed(column, 4 * pair + 2 * (1 - core) + sub)
             return column
 
         def finish(self):
-            self.sends(lambda step: self.copy(step).wait_send())
+            def sent(step):
+                for sub in range(2):
+                    self.copy(step, sub).wait_send()
+
+            self.sends(sent)
 
             def action():
                 for step in range(cols):
                     for pair in range(per // 2):
-                        self.forward(step, pair).wait_send()
+                        for sub in range(2):
+                            self.forward(step, pair, sub).wait_send()
 
             guard(self.active, action)
 
@@ -428,9 +443,9 @@
             vm((m, width), F32),
             vm((m, width), F32),
             vm((2, mk, width), F32),
-            dma((6, panels // 2)),
+            dma((6, panels // 2, 2)),
+            dma((6, cols, 2 * per)),
             dma((6, cols, per)),
-            dma((6, cols, per // 2)),
             dma((5, cols - 1)),
             dma((5, cols - 1)),
             dma((2,)),

time: 109 us -> 109 us (level)
  no operation moved by 1% of the time
where the time goes in v3:
time: 109 us
  Pallas kernels  104 us (95%)
  local copies, waits for them, and re-layouts  3.13 us (3%)
  other arithmetic  1.18 us (1%)
    pallas_call x1, Pallas kernels, shards(): pl.pallas_call(functools.partial(kernel, panels, cols), out_shape=(jax.Sh...  104 us
    unnamed x6, local copies, waits for them, and re-layouts  3.12 us

profile of v3, /device:TPU:24, one launch (start us, length us, event | category | flops | bytes accessed | tf_op | source)
XLA Modules:
  0.0 108.8 jit_solution(7091445133208747579)
XLA Ops:
  0.6 0.0 copy-start.1
  0.6 0.7 copy-done.1
  1.4 0.6 dynamic-slice_subtract_fusion.1.row_map
  1.9 0.6 dynamic-slice_subtract_fusion.col_map
  2.5 103.9 %shard_map.113 = (f32[512,128]{1,0:T(8,128)}, f32[2,256,128]{2,1,0:T(8,128)}) custom-call(f32[2,256,128]{2,1,0:T(8,128)} %pivot_rhs.1, f32[512,128]{1,0:T(8,128)} %update_rhs.1, f32[512,128]{1,0:T(8,128)} %parent_rhs.1, bf16[2,256,512]{2,1,0:T(8,128)(2,1)} %lower_pivot.1, bf16[512,512]{1,0:T(8,128)(2,1)} %lower_update.1, bf16[512,1024]{1,0:T(8,128)(2,1)} %parent_lower.1, ...), custom_call_target="tpu_custom_call" | custom-call | tf_op jit(solution)/shard_map/pallas_call | solution.py:416
  106.4 0.0 copy-start
  106.4 1.7 %copy.14 = f32[512,128]{1,0:T(8,128)} copy(f32[512,128]{1,0:T(8,128)} %get-tuple-element.4) | data formatting | bytes 524288
  108.1 0.0 copy-done
  108.1 0.7 copy.15
  (1 shorter events, 0.0 us)
Async XLA Ops:
  0.6 0.7 copy-start.1
  106.4 1.7 %copy-start = (f32[2,256,128]{2,1,0:T(8,128)S(1)}, f32[2,256,128]{2,1,0:T(8,128)}, u32[]{:S(2)}) copy-start(f32[2,256,128]{2,1,0:T(8,128)} %get-tuple-element.5) | copy-start | bytes 786436

commit v4 on v2

--- a/solution.py
+++ b/solution.py
@@ -177,7 +177,7 @@
 
         def pass_on(self):
             def action():
-                for step in range(cols):
+                for step in [last] + list(range(last)):
                     for pair in range(per // 2):
                         self.landed(lax.rem(me_r + 1 + step, cols), 2 * pair + core)
                         self.forward(step, pair).start()
@@ -231,6 +231,12 @@
                     self.copy(step).wait_send()
 
             guard(self.active, action)
+
+    def targets(ref, k, index, size, base):
+        if ref.shape[0] == 2:
+            return ref[k : k + 1, :]
+        start = pl.multiple_of(k * (ref.shape[1] // 2) + index * size, 128)
+        return ref[:, pl.ds(start, size)] - base
 
     def whole(panel):
         return None
@@ -259,7 +265,7 @@
     width = upper_update.shape[2]
     for k in range(2):
         rows = lax.broadcasted_iota(jnp.int32, (per * m, width), 0)
-        chosen = (rows == col_map[k : k + 1, :]).astype(F32).astype(BF)
+        chosen = (rows == targets(col_map, k, me_r, width, me_r * per * m)).astype(F32).astype(BF)
         picked[k] = lax.dot_general(
             upper_update[k], chosen, (((1,), (1,)), ((), ())), preferred_element_type=F32
         ).astype(BF)
@@ -320,7 +326,7 @@
     rows = lax.broadcasted_iota(jnp.int32, (m, m // 2), 0)
     for k in range(2):
         pltpu.make_async_copy(moved.at[k], moved.at[k], sh_recv.at[k]).wait()
-        chosen = (rows == row_map[k : k + 1, :]).astype(F32).astype(BF)
+        chosen = (rows == targets(row_map, k, me_p, m // 2, me_p * m)).astype(F32).astype(BF)
         spread_sum[...] += dot(chosen, moved[k])
     vec[0, 0] = spread_sum[...].astype(BF)
     g_low.start()
@@ -393,9 +399,15 @@
     per = panels // cols
     sides = maps.reshape(2, -1)
     me_p, me_r = lax.axis_index("panel"), lax.axis_index("rhs")
-    row_map = lax.dynamic_slice_in_dim(sides, me_p * (m // 2), m // 2, 1) - me_p * m
     wide = arrays[8].shape[2]
-    col_map = lax.dynamic_slice_in_dim(sides, me_r * wide, wide, 1) - me_r * per * m
+
+    def cut(index, size, base):
+        if size % 128 == 0:
+            return maps.reshape(1, -1)
+        return lax.dynamic_slice_in_dim(sides, index * size, size, 1) - base
+
+    row_map = cut(me_p, m // 2, me_p * m)
+    col_map = cut(me_r, wide, me_r * per * m)
     vm = pltpu.VMEM
     dma = pltpu.SemaphoreType.DMA
     return pl.pallas_call(

time: 109 us -> 108 us (level)
  Pallas kernels: 103 us -> 105 us
  other arithmetic: 1.18 us -> 0 us
    pallas_call x1, Pallas kernels: 103 us -> 105 us  [shards(): pl.pallas_call(functools.partial(kernel, panels, cols), out_shape=(jax.Sh...]
    sub x2 -> x0, other arithmetic: 1.18 us -> none  [the longest x1 0.6 us: shards(): lax.dynamic_slice_in_dim(sides, me_r * wide, wide, 1) - me_r * per * m]
    unnamed x6 -> x4, local copies, waits for them, and re-layouts: 3.12 us -> 2.42 us
where the time goes in v4:
time: 108 us
  Pallas kernels  105 us (97%)
  local copies, waits for them, and re-layouts  2.42 us (2%)
    pallas_call x1, Pallas kernels, shards(): pl.pallas_call(functools.partial(kernel, panels, cols), out_shape=(jax.Sh...  105 us
    unnamed x4, local copies, waits for them, and re-layouts  2.42 us

profile of v4, /device:TPU:24, one launch (start us, length us, event | category | flops | bytes accessed | tf_op | source)
XLA Modules:
  0.0 107.9 jit_solution(1938642734498128057)
XLA Ops:
  0.6 104.8 %shard_map.113 = (f32[512,128]{1,0:T(8,128)}, f32[2,256,128]{2,1,0:T(8,128)}) custom-call(f32[2,256,128]{2,1,0:T(8,128)} %pivot_rhs.1, f32[512,128]{1,0:T(8,128)} %update_rhs.1, f32[512,128]{1,0:T(8,128)} %parent_rhs.1, bf16[2,256,512]{2,1,0:T(8,128)(2,1)} %lower_pivot.1, bf16[512,512]{1,0:T(8,128)(2,1)} %lower_update.1, bf16[512,1024]{1,0:T(8,128)(2,1)} %parent_lower.1, ...), custom_call_target="tpu_custom_call" | custom-call | tf_op jit(solution)/shard_map/pallas_call | solution.py:413
  105.4 0.0 copy-start
  105.5 1.7 %copy.14 = f32[512,128]{1,0:T(8,128)} copy(f32[512,128]{1,0:T(8,128)} %get-tuple-element.4) | data formatting | bytes 524288
  107.2 0.0 copy-done
  107.2 0.7 copy.15
Async XLA Ops:
  105.4 1.7 %copy-start = (f32[2,256,128]{2,1,0:T(8,128)S(1)}, f32[2,256,128]{2,1,0:T(8,128)}, u32[]{:S(2)}) copy-start(f32[2,256,128]{2,1,0:T(8,128)} %get-tuple-element.5) | copy-start | bytes 786436
